TPU v7x, 32 devices: a whole 2x2x4 slice. The times are simulated.
32 devices in a mesh: dp: 8 (over y, x, core), tensor: 4 (over z).
Axes of the slice: x: 2, y: 2, z: 4, core: 2. Of those that a mesh axis runs over, the one named last changes fastest.
Arguments:
- tokens: bfloat16 [12288, 2048], P(('dp', 'tensor')), may hold values from -6 to 6
- segments: int32 [12288], P('dp'), may hold values from 0 to 4, as said below
- cotangent: bfloat16 [12288, 2048], P(('dp', 'tensor')), may hold values from -6 to 6
- ln1_gain: bfloat16 [2048], replicated, may hold values from 0.5 to 1.5
- ln1_shift: bfloat16 [2048], replicated, may hold values from -1.5 to 1.5
- w_query: bfloat16 [2048, 2048], P('dp', 'tensor'), may hold values from -0.1875 to 0.1875
- b_query: bfloat16 [2048], P('tensor'), may hold values from -1.5 to 1.5
- w_key: bfloat16 [2048, 2048], P('dp', 'tensor'), may hold values from -0.1875 to 0.1875
- w_value: bfloat16 [2048, 2048], P('dp', 'tensor'), may hold values from -0.125 to 0.125
- b_value: bfloat16 [2048], P('tensor'), may hold values from -1.5 to 1.5
- w_out: bfloat16 [2048, 2048], P('tensor', 'dp'), may hold values from -0.5 to 0.5
- b_out: bfloat16 [2048], replicated, may hold values from -1.5 to 1.5
- ln2_gain: bfloat16 [2048], replicated, may hold values from 0.5 to 1.5
- ln2_shift: bfloat16 [2048], replicated, may hold values from -1.5 to 1.5
- w_up: bfloat16 [2048, 8192], P('dp', 'tensor'), may hold values from -0.125 to 0.125
- b_up: bfloat16 [8192], P('tensor'), may hold values from -1.5 to 1.5
- w_down: bfloat16 [8192, 2048], P('tensor', 'dp'), may hold values from -0.0625 to 0.0625
- b_down: bfloat16 [2048], replicated, may hold values from -1.5 to 1.5
Outputs:
- output: bfloat16 [12288, 2048], P(('dp', 'tensor'))
- input_grad: bfloat16 [12288, 2048], P(('dp', 'tensor'))
- grad_ln1_gain: float32 [2048], replicated
- grad_ln1_shift: float32 [2048], replicated
- grad_w_query: float32 [2048, 2048], P('dp', 'tensor')
- grad_b_query: float32 [2048], P('tensor')
- grad_w_key: float32 [2048, 2048], P('dp', 'tensor')
- grad_w_value: float32 [2048, 2048], P('dp', 'tensor')
- grad_b_value: float32 [2048], P('tensor')
- grad_w_out: float32 [2048, 2048], P('tensor', 'dp')
- grad_b_out: float32 [2048], replicated
- grad_ln2_gain: float32 [2048], replicated
- grad_ln2_shift: float32 [2048], replicated
- grad_w_up: float32 [2048, 8192], P('dp', 'tensor')
- grad_b_up: float32 [8192], P('tensor')
- grad_w_down: float32 [8192, 2048], P('tensor', 'dp')
- grad_b_down: float32 [2048], replicated
Inputs may be any that keep to these rules, and one draw needn't show every extreme that they name: Within each group of 1536 tokens the first 1024 have segment 0; the rest form 4 contiguous runs with segments 1 to 4 in rising order, each run 128 // 2 to 192 tokens long; in every group one run is exactly 192 long.
All inputs are finite; a program needn't handle non-finite values.
Results may differ from a plain program's by a relative error of at most 0.017.
Values may be sent and summed in bfloat16 or wider, within the bound.
A program may use at most 320 MiB of HBM per device.

v0:
```python
import math
import jax
import jax.numpy as jnp
from jax import lax
from jax.sharding import PartitionSpec as P

HDIM = 128
QBLK = 768
EPS = 1e-05
NEG = -1e30


def layer_norm(values, norm_gain, norm_shift):
    row_mean = jnp.mean(values, axis=-1, keepdims=True)
    centred = values - row_mean
    row_var = jnp.mean(centred * centred, axis=-1, keepdims=True)
    return centred * lax.rsqrt(row_var + EPS) * norm_gain + norm_shift


def gelu_exact(values):
    return jax.nn.gelu(values, approximate=False)


def row_dot(left_side, right_side):
    return jnp.dot(left_side, right_side, preferred_element_type=jnp.float32)


def left_dot(left_side, right_side):
    return lax.dot_general(
        left_side, right_side, (((0,), (0,)), ((), ())), preferred_element_type=jnp.float32
    )


def back_dot(left_side, right_side):
    return lax.dot_general(
        left_side, right_side, (((1,), (1,)), ((), ())), preferred_element_type=jnp.float32
    )


def visible(segments, first_row, row_count, key_end):
    query_pos = first_row + jnp.arange(row_count)
    key_pos = jnp.arange(key_end)
    seg_query = segments[first_row : first_row + row_count]
    seg_key = segments[:key_end]
    causal = key_pos[None, :] <= query_pos[:, None]
    shared = (seg_key[None, :] == seg_query[:, None]) | (seg_key[None, :] == 0)
    return causal & shared


def attend_block(queries, key_rows, value_rows, allowed):
    scores = jnp.einsum("qhd,khd->hqk", queries, key_rows, preferred_element_type=jnp.float32)
    scores = jnp.where(allowed[None], scores, NEG)
    row_top = jnp.max(scores, axis=-1, keepdims=True)
    raised = jnp.exp(scores - row_top)
    row_total = jnp.sum(raised, axis=-1, keepdims=True)
    weights = raised / row_total
    mixed = jnp.einsum(
        "hqk,khd->qhd", weights.astype(jnp.bfloat16), value_rows, preferred_element_type=jnp.float32
    )
    return (mixed.astype(jnp.bfloat16), row_top + jnp.log(row_total))


def attend_back(queries, key_rows, value_rows, grad_out, log_total, allowed):
    scores = jnp.einsum("qhd,khd->hqk", queries, key_rows, preferred_element_type=jnp.float32)
    weights = jnp.where(allowed[None], jnp.exp(scores - log_total), 0.0)
    grad_weights = jnp.einsum(
        "qhd,khd->hqk", grad_out, value_rows, preferred_element_type=jnp.float32
    )
    inner = jnp.sum(weights * grad_weights, axis=-1, keepdims=True)
    grad_scores = (weights * (grad_weights - inner)).astype(jnp.bfloat16)
    grad_query = jnp.einsum(
        "hqk,khd->qhd", grad_scores, key_rows, preferred_element_type=jnp.float32
    )
    grad_key = jnp.einsum("hqk,qhd->khd", grad_scores, queries, preferred_element_type=jnp.float32)
    grad_value = jnp.einsum(
        "hqk,qhd->khd", weights.astype(jnp.bfloat16), grad_out, preferred_element_type=jnp.float32
    )
    return (grad_query, grad_key, grad_value)


def on_device(
    tokens,
    segments,
    cotangent,
    ln1_gain,
    ln1_shift,
    w_query,
    b_query,
    w_key,
    w_value,
    b_value,
    w_out,
    b_out,
    ln2_gain,
    ln2_shift,
    w_up,
    b_up,
    w_down,
    b_down,
):
    score_scale = 1.0 / math.sqrt(HDIM)
    full_query, full_key, full_value, full_out, full_up, full_down = (
        lax.all_gather(w_query, "dp", axis=0, tiled=True),
        lax.all_gather(w_key, "dp", axis=0, tiled=True),
        lax.all_gather(w_value, "dp", axis=0, tiled=True),
        lax.all_gather(w_out, "dp", axis=1, tiled=True),
        lax.all_gather(w_up, "dp", axis=0, tiled=True),
        lax.all_gather(w_down, "dp", axis=1, tiled=True),
    )
    group_len = segments.shape[0]
    head_cols = full_query.shape[1]
    heads_here = head_cols // HDIM
    block_count = group_len // QBLK
    inputs = tokens.astype(jnp.float32)
    normed_one, norm_one_back = jax.vjp(
        layer_norm, inputs, ln1_gain.astype(jnp.float32), ln1_shift.astype(jnp.float32)
    )
    h_one = normed_one.astype(jnp.bfloat16)
    h_one_full = lax.all_gather(h_one, "tensor", axis=0, tiled=True)
    w_qkv = jnp.concatenate([full_query, full_key, full_value], axis=1)
    w_kv = w_qkv[:, head_cols:]
    projected = row_dot(h_one_full, w_qkv)
    queries = ((projected[:, :head_cols] + b_query.astype(jnp.float32)) * score_scale).astype(
        jnp.bfloat16
    )
    key_rows = projected[:, head_cols : 2 * head_cols].astype(jnp.bfloat16)
    value_rows = (projected[:, 2 * head_cols :] + b_value.astype(jnp.float32)).astype(jnp.bfloat16)
    query3 = queries.reshape(group_len, heads_here, HDIM)
    key3 = key_rows.reshape(group_len, heads_here, HDIM)
    value3 = value_rows.reshape(group_len, heads_here, HDIM)
    pieces = []
    totals = []
    for block in range(block_count):
        first_row = block * QBLK
        key_end = first_row + QBLK
        allowed = visible(segments, first_row, QBLK, key_end)
        mixed_block, log_total = attend_block(
            query3[first_row:key_end], key3[:key_end], value3[:key_end], allowed
        )
        pieces.append(mixed_block)
        totals.append(log_total)
    attended = jnp.concatenate(pieces, axis=0).reshape(group_len, head_cols)
    resid = (
        inputs
        + lax.psum_scatter(row_dot(attended, full_out), "tensor", scatter_dimension=0, tiled=True)
        + b_out.astype(jnp.float32)
    )
    normed_two, norm_two_back = jax.vjp(
        layer_norm, resid, ln2_gain.astype(jnp.float32), ln2_shift.astype(jnp.float32)
    )
    h_two = normed_two.astype(jnp.bfloat16)
    h_two_full = lax.all_gather(h_two, "tensor", axis=0, tiled=True)
    pre_act = row_dot(h_two_full, full_up) + b_up.astype(jnp.float32)
    activated, gelu_back = jax.vjp(gelu_exact, pre_act)
    act_low = activated.astype(jnp.bfloat16)
    output = (
        resid
        + lax.psum_scatter(
            row_dot(act_low, full_down).astype(jnp.bfloat16),
            "tensor",
            scatter_dimension=0,
            tiled=True,
        ).astype(jnp.float32)
        + b_down.astype(jnp.float32)
    ).astype(jnp.bfloat16)
    grad_y = cotangent.astype(jnp.float32)
    grad_y_full = lax.all_gather(cotangent, "tensor", axis=0, tiled=True)
    grad_down = left_dot(act_low, grad_y_full)
    grad_act = back_dot(grad_y_full, full_down)
    grad_pre = gelu_back(grad_act)[0].astype(jnp.bfloat16)
    grad_bias_up = jnp.sum(grad_pre.astype(jnp.float32), axis=0)
    grad_up = left_dot(h_two_full, grad_pre)
    grad_h_two = lax.psum_scatter(
        back_dot(grad_pre, full_up), "tensor", scatter_dimension=0, tiled=True
    )
    grad_resid_norm, grad_gain_two, grad_shift_two = norm_two_back(grad_h_two)
    grad_resid = grad_y + grad_resid_norm
    grad_mix = grad_resid.astype(jnp.bfloat16)
    grad_bias_out = jnp.sum(grad_mix.astype(jnp.float32), axis=0)
    grad_bias_down = jnp.sum(grad_y, axis=0)
    grad_mix_full = lax.all_gather(grad_mix, "tensor", axis=0, tiled=True)
    grad_out_w = left_dot(attended, grad_mix_full)
    grad_att = (
        back_dot(grad_mix_full, full_out).astype(jnp.bfloat16).reshape(group_len, heads_here, HDIM)
    )
    grad_key_sum = jnp.zeros((group_len, heads_here, HDIM), jnp.float32)
    grad_value_sum = jnp.zeros((group_len, heads_here, HDIM), jnp.float32)
    query_grads = []
    for block in range(block_count):
        first_row = block * QBLK
        key_end = first_row + QBLK
        allowed = visible(segments, first_row, QBLK, key_end)
        grad_q_block, grad_k_part, grad_v_part = attend_back(
            query3[first_row:key_end],
            key3[:key_end],
            value3[:key_end],
            grad_att[first_row:key_end],
            totals[block],
            allowed,
        )
        query_grads.append(grad_q_block.astype(jnp.bfloat16))
        grad_key_sum = grad_key_sum.at[:key_end].add(grad_k_part)
        grad_value_sum = grad_value_sum.at[:key_end].add(grad_v_part)
    grad_q = jnp.concatenate(query_grads, axis=0).reshape(group_len, head_cols)
    grad_k = grad_key_sum.reshape(group_len, head_cols).astype(jnp.bfloat16)
    grad_v = grad_value_sum.reshape(group_len, head_cols).astype(jnp.bfloat16)
    grad_qkv = jnp.concatenate([grad_q, grad_k, grad_v], axis=1)
    grad_qkv_w = left_dot(h_one_full, grad_qkv)
    grad_wq = grad_qkv_w[:, :head_cols] * score_scale
    grad_wk = grad_qkv_w[:, head_cols : 2 * head_cols]
    grad_wv = grad_qkv_w[:, 2 * head_cols :]
    grad_bias_query = jnp.sum(grad_q.astype(jnp.float32), axis=0) * score_scale
    grad_bias_value = jnp.sum(grad_v.astype(jnp.float32), axis=0)
    grad_h_one = lax.psum_scatter(
        (
            back_dot(grad_qkv[:, :head_cols], full_query) * score_scale
            + back_dot(grad_qkv[:, head_cols:], w_kv)
        ).astype(jnp.bfloat16),
        "tensor",
        scatter_dimension=0,
        tiled=True,
    ).astype(jnp.float32)
    grad_in_norm, grad_gain_one, grad_shift_one = norm_one_back(grad_h_one)
    input_grad = (grad_resid + grad_in_norm).astype(jnp.bfloat16)
    sent_query, sent_key, sent_value, sent_out, sent_up, sent_down = (
        lax.psum_scatter(
            grad_wq.astype(jnp.bfloat16), "dp", scatter_dimension=0, tiled=True
        ).astype(jnp.float32),
        lax.psum_scatter(
            grad_wk.astype(jnp.bfloat16), "dp", scatter_dimension=0, tiled=True
        ).astype(jnp.float32),
        lax.psum_scatter(
            grad_wv.astype(jnp.bfloat16), "dp", scatter_dimension=0, tiled=True
        ).astype(jnp.float32),
        lax.psum_scatter(
            grad_out_w.astype(jnp.bfloat16), "dp", scatter_dimension=1, tiled=True
        ).astype(jnp.float32),
        lax.psum_scatter(
            grad_up.astype(jnp.bfloat16), "dp", scatter_dimension=0, tiled=True
        ).astype(jnp.float32),
        lax.psum_scatter(
            grad_down.astype(jnp.bfloat16), "dp", scatter_dimension=1, tiled=True
        ).astype(jnp.float32),
    )
    summed_query, summed_value, summed_up = lax.psum(
        (grad_bias_query, grad_bias_value, grad_bias_up), "dp"
    )
    gain_one_sum, shift_one_sum, gain_two_sum, shift_two_sum, bias_out_sum, bias_down_sum = (
        lax.psum(
            (
                grad_gain_one,
                grad_shift_one,
                grad_gain_two,
                grad_shift_two,
                grad_bias_out,
                grad_bias_down,
            ),
            ("dp", "tensor"),
        )
    )
    return (
        output,
        input_grad,
        gain_one_sum,
        shift_one_sum,
        sent_query,
        summed_query,
        sent_key,
        sent_value,
        summed_value,
        sent_out,
        bias_out_sum,
        gain_two_sum,
        shift_two_sum,
        sent_up,
        summed_up,
        sent_down,
        bias_down_sum,
    )


def solution(mesh):
    return jax.shard_map(
        on_device,
        mesh=mesh,
        in_specs=(
            P(("dp", "tensor"), None),
            P("dp"),
            P(("dp", "tensor"), None),
            P(),
            P(),
            P("dp", "tensor"),
            P("tensor"),
            P("dp", "tensor"),
            P("dp", "tensor"),
            P("tensor"),
            P("tensor", "dp"),
            P(),
            P(),
            P(),
            P("dp", "tensor"),
            P("tensor"),
            P("tensor", "dp"),
            P(),
        ),
        out_specs=(
            P(("dp", "tensor"), None),
            P(("dp", "tensor"), None),
            P(),
            P(),
            P("dp", "tensor"),
            P("tensor"),
            P("dp", "tensor"),
            P("dp", "tensor"),
            P("tensor"),
            P("tensor", "dp"),
            P(),
            P(),
            P(),
            P("dp", "tensor"),
            P("tensor"),
            P("tensor", "dp"),
            P(),
        ),
        check_vma=False,
    )
```

profile of v0, /device:TPU:0, one launch (start us, length us, event | category | flops | bytes accessed | tf_op | source)
XLA Modules:
  0.0 1852.3 jit_solution(1122255741000545251)
XLA Ops:
  19.8 20.7 %all-gather.13.cloned.1.call-done = bf16[2048,512]{1,0:T(8,128)(2,1)} async-done(((bf16[256,512]{1,0:T(8,128)(2,1)}), bf16[2048,512]{1,0:T(8,128)(2,1)}) %all-gather.13.cloned.1.call-update) | async-done | bytes 2097168 | tf_op jit(solution)/shard_map/all_gather | solution.py:103
  40.5 29.7 %all-gather.15.cloned.1.call-done = bf16[2048,512]{1,0:T(8,128)(2,1)} async-done(((bf16[256,512]{1,0:T(8,128)(2,1)}), bf16[2048,512]{1,0:T(8,128)(2,1)}) %all-gather.15.cloned.1.call-update) | async-done | bytes 2097168 | tf_op jit(solution)/shard_map/all_gather | solution.py:104
  70.2 29.7 %all-gather.17.cloned.1.call-done = bf16[2048,512]{1,0:T(8,128)(2,1)} async-done(((bf16[256,512]{1,0:T(8,128)(2,1)}), bf16[2048,512]{1,0:T(8,128)(2,1)}) %all-gather.17.cloned.1.call-update) | async-done | bytes 2097168 | tf_op jit(solution)/shard_map/all_gather | solution.py:105
  99.9 117.4 %all-gather.11.cloned.1.call-done = bf16[1536,2048]{1,0:T(8,128)(2,1)} async-done(((bf16[384,2048]{1,0:T(8,128)(2,1)}), bf16[1536,2048]{1,0:T(8,128)(2,1)}) %all-gather.11.cloned.1.call-update) | async-done | bytes 6291472 | tf_op jit(solution)/shard_map/all_gather | solution.py:119
  217.2 17.0 fusion.99
  237.3 3.9 fusion.60
  247.8 3.8 fusion.80
  251.6 4.3 select_reduce_fusion
  255.8 5.1 fusion
  262.6 9.2 fusion.79
  272.0 8.5 fusion.101
  281.5 209.5 %reduce-scatter.11.cloned.1.call-done = f32[384,2048]{1,0:T(8,128)} async-done(((f32[1536,2048]{1,0:T(8,128)}), f32[384,2048]{1,0:T(8,128)}) %reduce-scatter.11.cloned.1.call-update) | async-done | bytes 3145744 | tf_op jit(solution)/shard_map/reduce_scatter | solution.py:145
  498.7 49.4 %all-gather.23.cloned.1.call-done = bf16[2048,2048]{1,0:T(8,128)(2,1)} async-done(((bf16[256,2048]{1,0:T(8,128)(2,1)}), bf16[2048,2048]{1,0:T(8,128)(2,1)}) %all-gather.23.cloned.1.call-update) | async-done | bytes 8388624 | tf_op jit(solution)/shard_map/all_gather | solution.py:107
  548.2 117.5 %all-gather.21.cloned.1.call-done = bf16[1536,2048]{1,0:T(8,128)(2,1)} async-done(((bf16[384,2048]{1,0:T(8,128)(2,1)}), bf16[1536,2048]{1,0:T(8,128)(2,1)}) %all-gather.21.cloned.1.call-update) | async-done | bytes 6291472 | tf_op jit(solution)/shard_map/all_gather | solution.py:152
  665.7 19.1 %fusion.102 = f32[1536,2048]{1,0:T(8,128)} fusion(bf16[1536,2048]{1,0:T(8,128)(2,1)} %all-gather.21.cloned.1.call-done, bf16[2048,2048]{1,0:T(8,128)(2,1)} %all-gather.23.cloned.1.call-done), kind=kOutput, calls=%fused_computation.163 | convolution fusion | flops 12884901888 | bytes 27262976 | tf_op jit(solution)/shard_map/dot_general | solution.py:25
  684.8 96.0 %all-gather.27.cloned.1.call-done = bf16[1536,2048]{1,0:T(8,128)(2,1)} async-done(((bf16[384,2048]{1,0:T(8,128)(2,1)}), bf16[1536,2048]{1,0:T(8,128)(2,1)}) %all-gather.27.cloned.1.call-update) | async-done | bytes 6291472 | tf_op jit(solution)/shard_map/all_gather | solution.py:167
  780.8 55.8 %all-gather.25.cloned.1.call-done = bf16[2048,2048]{1,0:T(8,128)(2,1)} async-done(((bf16[2048,256]{1,0:T(8,128)(2,1)}), bf16[2048,2048]{1,0:T(8,128)(2,1)}) %all-gather.25.cloned.1.call-update) | async-done | bytes 8388624 | tf_op jit(solution)/shard_map/all_gather | solution.py:108
  836.6 48.6 %convert_reduce_fusion = (f32[2048]{0:T(1024)}, bf16[1536,2048]{1,0:T(8,128)(2,1)S(1)}, f32[1536,2048]{1,0:T(8,128)}) fusion(f32[1536,2048]{1,0:T(8,128)} %fusion.102, f32[2048]{0:T(1024)S(1)} %convert_element_type.195, bf16[1536,2048]{1,0:T(8,128)(2,1)} %all-gather.27.cloned.1.call-done, bf16[2048,2048]{1,0:T(8,128)(2,1)} %all-gather.25.cloned.1.call-done), kind=kOutput, calls=%fused_computation.9 | convolution fusion | flops 13120829440 | bytes 46153728 | tf_op jit(solution)/shard_map/dot_general | solution.py:35
  887.8 18.3 fusion.103
  906.1 10.7 multiply_convert_fusion.1
  919.6 17.5 convolution_convert_fusion.2
  937.8 180.3 %reduce-scatter.15.cloned.1.call-done = f32[384,2048]{1,0:T(8,128)} async-done(((f32[1536,2048]{1,0:T(8,128)}), f32[384,2048]{1,0:T(8,128)}) %reduce-scatter.15.cloned.1.call-update) | async-done | bytes 3145744 | tf_op jit(solution)/shard_map/reduce_scatter | solution.py:173
  1121.7 110.5 %reduce-scatter.13.cloned.1.call-done = bf16[384,2048]{1,0:T(8,128)(2,1)} async-done(((bf16[1536,2048]{1,0:T(8,128)(2,1)}), bf16[384,2048]{1,0:T(8,128)(2,1)}) %reduce-scatter.13.cloned.1.call-update) | async-done | bytes 1572880 | tf_op jit(solution)/shard_map/reduce_scatter | solution.py:158
  1232.2 4.8 fusion.92
  1241.0 19.4 %convolution_convert_fusion = bf16[2048,2048]{1,0:T(8,128)(2,1)} fusion(bf16[1536,2048]{1,0:T(8,128)(2,1)} %copy-done.28, bf16[1536,2048]{1,0:T(8,128)(2,1)} %all-gather.27.cloned.1.call-done), kind=kOutput, calls=%fused_computation.39 | convolution fusion | flops 12889096192 | bytes 20971520 | tf_op jit(solution)/shard_map/dot_general | solution.py:29
  1260.6 19.3 %convolution_convert_fusion.1 = bf16[2048,2048]{1,0:T(8,128)(2,1)} fusion(bf16[1536,2048]{1,0:T(8,128)(2,1)} %all-gather.21.cloned.1.call-done, bf16[1536,2048]{1,0:T(8,128)(2,1)} %copy-done.78), kind=kOutput, calls=%fused_computation.40 | convolution fusion | flops 12889096192 | bytes 20971520 | tf_op jit(solution)/shard_map/dot_general | solution.py:29
  1280.7 76.2 %all-gather.29.cloned.1.call-done = bf16[1536,2048]{1,0:T(8,128)(2,1)} async-done(((bf16[384,2048]{1,0:T(8,128)(2,1)}), bf16[1536,2048]{1,0:T(8,128)(2,1)}) %all-gather.29.cloned.1.call-update) | async-done | bytes 6291472 | tf_op jit(solution)/shard_map/all_gather | solution.py:181
  1356.9 6.9 convolution_convert_fusion.4
  1364.7 9.7 multiply_reduce_fusion.1
  1374.4 10.9 multiply_convert_fusion.2
  1385.3 4.2 fusion.77
  1392.3 17.0 multiply_reduce_fusion
  1409.3 14.8 multiply_convert_fusion
  1426.7 4.1 fusion.78
  1430.8 4.4 fusion.72
  1435.2 7.4 convolution_convert_fusion.3
  1442.6 14.6 convert_reduce_fusion.5
  1459.2 15.3 fusion.100
  1477.4 4.2 fusion.39
  1481.7 12.1 fusion.40
  1493.9 8.4 add_convert_fusion
  1508.3 24.5 %all-reduce.3 = (f32[512]{0:T(512)}, f32[512]{0:T(512)}, f32[2048]{0:T(1024)}) all-reduce(f32[512]{0:T(512)S(1)} %multiply_bitcast_fusion, f32[512]{0:T(512)S(1)} %bitcast.105, f32[2048]{0:T(1024)S(1)} %copy-done.69), channel_id=1, replica_groups=mesh['dp'=8,'tensor'=4] {'dp'}, use_global_device_ids=true, to_apply=%region_24.25 | all-reduce | flops 3072 | bytes 24576 | tf_op jit(solution)/shard_map/psum | solution.py:245
  1532.8 16.1 reduce-scatter.25.cloned.1.call-done
  1550.7 42.5 %reduce-scatter.21.cloned.1.call-done = bf16[256,512]{1,0:T(8,128)(2,1)} async-done(((bf16[2048,512]{1,0:T(8,128)(2,1)}), bf16[256,512]{1,0:T(8,128)(2,1)}) %reduce-scatter.21.cloned.1.call-update) | async-done | bytes 262160 | tf_op jit(solution)/shard_map/reduce_scatter | solution.py:229
  1595.0 42.5 %reduce-scatter.23.cloned.1.call-done = bf16[256,512]{1,0:T(8,128)(2,1)} async-done(((bf16[2048,512]{1,0:T(8,128)(2,1)}), bf16[256,512]{1,0:T(8,128)(2,1)}) %reduce-scatter.23.cloned.1.call-update) | async-done | bytes 262160 | tf_op jit(solution)/shard_map/reduce_scatter | solution.py:232
  1639.3 42.6 %reduce-scatter.19.cloned.1.call-done = bf16[256,512]{1,0:T(8,128)(2,1)} async-done(((bf16[2048,512]{1,0:T(8,128)(2,1)}), bf16[256,512]{1,0:T(8,128)(2,1)}) %reduce-scatter.19.cloned.1.call-update) | async-done | bytes 262160 | tf_op jit(solution)/shard_map/reduce_scatter | solution.py:226
  1683.7 111.2 %reduce-scatter.17.cloned.1.call-done = bf16[384,2048]{1,0:T(8,128)(2,1)} async-done(((bf16[1536,2048]{1,0:T(8,128)(2,1)}), bf16[384,2048]{1,0:T(8,128)(2,1)}) %reduce-scatter.17.cloned.1.call-update) | async-done | bytes 1572880 | tf_op jit(solution)/shard_map/reduce_scatter | solution.py:214
  1803.2 42.0 %all-reduce.2 = (f32[2048]{0:T(1024)}, f32[2048]{0:T(1024)}, f32[2048]{0:T(1024)}, f32[2048]{0:T(1024)}, f32[2048]{0:T(1024)}, /*index=5*/f32[2048]{0:T(1024)}) all-reduce(f32[2048]{0:T(1024)S(1)} %get-tuple-element.83, f32[2048]{0:T(1024)S(1)} %get-tuple-element.86, ...), channel_id=1, replica_groups=mesh['dp'=8,'tensor'=4] {'dp','tensor'}, use_global_device_ids=true, to_apply=%region_19.20 | all-reduce | flops 12288 | bytes 98304 | tf_op jit(solution)/shard_map/psum | solution.py:249
  (263 shorter events, 79.7 us)
Async XLA Ops:
  7.2 9.9 copy-start.76
  7.2 33.2 %all-gather.13.cloned.1.call-start = ((), (), s32[]{:S(2)}) async-start(), calls=%async_computation.11 | async-start | bytes 2359296 | tf_op jit(solution)/shard_map/all_gather | solution.py:103
  8.0 62.2 %all-gather.15.cloned.1.call-start = ((), (), s32[]{:S(2)}) async-start(), calls=%async_computation.12 | async-start | bytes 2359296 | tf_op jit(solution)/shard_map/all_gather | solution.py:104
  8.7 91.2 %all-gather.17.cloned.1.call-start = ((), (), s32[]{:S(2)}) async-start(), calls=%async_computation.13 | async-start | bytes 2359296 | tf_op jit(solution)/shard_map/all_gather | solution.py:105
  9.4 207.8 %all-gather.11.cloned.1.call-start = ((), (), s32[]{:S(2)}) async-start(), calls=%async_computation.10 | async-start | bytes 7864320 | tf_op jit(solution)/shard_map/all_gather | solution.py:119
  16.4 255.6 %all-gather.19.cloned.1.call-start = ((), (), s32[]{:S(2)}) async-start(), calls=%async_computation.14 | async-start | bytes 2359296 | tf_op jit(solution)/shard_map/all_gather | solution.py:106
  17.0 473.9 %reduce-scatter.11.cloned.1.call-start = ((), (), s32[]{:S(2)}) async-start(), calls=%async_computation.15 | async-start | bytes 15728640 | tf_op jit(solution)/shard_map/reduce_scatter | solution.py:145
  17.6 228.3 %copy-start.13 = (pred[768,768]{0,1:T(8,128)(4,1)}, pred[768,768]{0,1:T(8,128)(4,1)S(1)}, u32[]{:S(2)}) copy-start(pred[768,768]{0,1:T(8,128)(4,1)S(1)} %fusion.69) | copy-start | bytes 1769476
  19.8 242.5 %copy-start.6 = (pred[768,1536]{1,0:T(8,128)(4,1)}, pred[768,1536]{1,0:T(8,128)(4,1)S(1)}, u32[]{:S(2)}) copy-start(pred[768,1536]{1,0:T(8,128)(4,1)S(1)} %fusion.36) | copy-start | bytes 3538948
  237.3 14.3 copy-start.11
  241.2 21.1 %copy-start.15 = (bf16[1536,512]{0,1:T(8,128)(2,1)}, bf16[1536,512]{0,1:T(8,128)(2,1)S(1)}, u32[]{:S(2)}) copy-start(bf16[1536,512]{0,1:T(8,128)(2,1)S(1)} %get-tuple-element.107) | copy-start | bytes 4718596
  280.6 267.6 %all-gather.23.cloned.1.call-start = ((), (), s32[]{:S(2)}) async-start(), calls=%async_computation.17 | async-start | bytes 9437184 | tf_op jit(solution)/shard_map/all_gather | solution.py:107
  281.3 384.3 %all-gather.21.cloned.1.call-start = ((), (), s32[]{:S(2)}) async-start(), calls=%async_computation.16 | async-start | bytes 7864320 | tf_op jit(solution)/shard_map/all_gather | solution.py:152
  281.4 213.3 %copy-start.41 = (f32[2048]{0:T(1024)}, f32[2048]{0:T(1024)S(1)}, u32[]{:S(2)}) copy-start(f32[2048]{0:T(1024)S(1)} %convert_element_type.192) | copy-start | bytes 24580
  497.4 283.4 %all-gather.27.cloned.1.call-start = ((), (), s32[]{:S(2)}) async-start(), calls=%async_computation.20 | async-start | bytes 7864320 | tf_op jit(solution)/shard_map/all_gather | solution.py:167
  498.1 338.5 %all-gather.25.cloned.1.call-start = ((), (), s32[]{:S(2)}) async-start(), calls=%async_computation.18 | async-start | bytes 9437184 | tf_op jit(solution)/shard_map/all_gather | solution.py:108
  498.7 619.5 %reduce-scatter.15.cloned.1.call-start = ((), (), s32[]{:S(2)}) async-start(), calls=%async_computation.21 | async-start | bytes 15728640 | tf_op jit(solution)/shard_map/reduce_scatter | solution.py:173
  906.1 326.1 %reduce-scatter.13.cloned.1.call-start = ((), (), s32[]{:S(2)}) async-start(), calls=%async_computation.19 | async-start | bytes 7864320 | tf_op jit(solution)/shard_map/reduce_scatter | solution.py:158
  937.1 181.0 %copy-start.3 = (f32[384,2048]{1,0:T(8,128)S(1)}, f32[384,2048]{1,0:T(8,128)}, u32[]{:S(2)}) copy-start(f32[384,2048]{1,0:T(8,128)} %copy-done.2) | copy-start | bytes 9437188
  937.1 181.0 %copy-start.42 = (f32[2048]{0:T(1024)S(1)}, f32[2048]{0:T(1024)}, u32[]{:S(2)}) copy-start(f32[2048]{0:T(1024)} %copy-done.41) | copy-start | bytes 24580
  937.1 181.0 %copy-start.51 = (f32[384]{0:T(512)S(1)}, f32[384]{0:T(512)}, u32[]{:S(2)}) copy-start(f32[384]{0:T(512)} %copy-done.50) | copy-start | bytes 4612
  937.1 181.0 %copy-start.62 = (f32[384]{0:T(512)S(1)}, f32[384]{0:T(512)}, u32[]{:S(2)}) copy-start(f32[384]{0:T(512)} %copy-done.61) | copy-start | bytes 4612
  937.2 184.5 %copy-start.68 = (f32[384]{0:T(512)S(1)}, f32[384]{0:T(512)}, u32[]{:S(2)}) copy-start(f32[384]{0:T(512)} %copy-done.67) | copy-start | bytes 4612
  937.2 419.7 %all-gather.29.cloned.1.call-start = ((), (), s32[]{:S(2)}) async-start(), calls=%async_computation.22 | async-start | bytes 7864320 | tf_op jit(solution)/shard_map/all_gather | solution.py:181
  1240.9 261.4 %reduce-scatter.29.cloned.1.call-start = ((), (), s32[]{:S(2)}) async-start(), calls=%async_computation.29 | async-start | bytes 9437184 | tf_op jit(solution)/shard_map/reduce_scatter | solution.py:241
  1260.4 244.7 %reduce-scatter.27.cloned.1.call-start = ((), (), s32[]{:S(2)}) async-start(), calls=%async_computation.28 | async-start | bytes 9437184 | tf_op jit(solution)/shard_map/reduce_scatter | solution.py:238
  1280.0 268.9 %reduce-scatter.25.cloned.1.call-start = ((), (), s32[]{:S(2)}) async-start(), calls=%async_computation.27 | async-start | bytes 2359296 | tf_op jit(solution)/shard_map/reduce_scatter | solution.py:235
  1280.7 84.0 %copy-start.14 = (pred[768,768]{0,1:T(8,128)(4,1)S(1)}, pred[768,768]{0,1:T(8,128)(4,1)}, u32[]{:S(2)}) copy-start(pred[768,768]{0,1:T(8,128)(4,1)} %copy-done.13) | copy-start | bytes 1769476
  1280.7 84.0 %copy-start.31 = (bf16[768,512]{0,1:T(8,128)(2,1)S(1)}, bf16[768,512]{0,1:T(8,128)(2,1)}, u32[]{:S(2)}) copy-start(bf16[768,512]{0,1:T(8,128)(2,1)} %copy-done.30) | copy-start | bytes 2359300
  1374.4 10.9 copy-start.21
  1409.3 14.8 copy-start.22
  1409.3 14.8 copy-start.27
  1442.6 14.7 copy-start.23
  1442.6 14.7 copy-start.26
  1457.2 136.0 %reduce-scatter.21.cloned.1.call-start = ((), (), s32[]{:S(2)}) async-start(), calls=%async_computation.25 | async-start | bytes 2359296 | tf_op jit(solution)/shard_map/reduce_scatter | solution.py:229
  1457.4 17.1 copy-start.36
  1476.8 160.7 %reduce-scatter.23.cloned.1.call-start = ((), (), s32[]{:S(2)}) async-start(), calls=%async_computation.26 | async-start | bytes 2359296 | tf_op jit(solution)/shard_map/reduce_scatter | solution.py:232
  1477.4 204.5 %reduce-scatter.19.cloned.1.call-start = ((), (), s32[]{:S(2)}) async-start(), calls=%async_computation.24 | async-start | bytes 2359296 | tf_op jit(solution)/shard_map/reduce_scatter | solution.py:226
  1481.7 313.2 %reduce-scatter.17.cloned.1.call-start = ((), (), s32[]{:S(2)}) async-start(), calls=%async_computation.23 | async-start | bytes 7864320 | tf_op jit(solution)/shard_map/reduce_scatter | solution.py:214
  1481.7 12.2 copy-start.37
  1481.7 12.2 copy-start.77
  1505.0 289.9 %copy-start.5 = (bf16[384,2048]{1,0:T(8,128)(2,1)S(1)}, bf16[384,2048]{1,0:T(8,128)(2,1)}, u32[]{:S(2)}) copy-start(bf16[384,2048]{1,0:T(8,128)(2,1)} %param.30) | copy-start | bytes 4718596
  1505.0 289.9 %copy-start.40 = (f32[2048]{0:T(1024)S(1)}, f32[2048]{0:T(1024)}, u32[]{:S(2)}) copy-start(f32[2048]{0:T(1024)} %copy-done.39) | copy-start | bytes 24580
  1505.0 289.9 %copy-start.49 = (f32[384]{0:T(512)S(1)}, f32[384]{0:T(512)}, u32[]{:S(2)}) copy-start(f32[384]{0:T(512)} %copy-done.48) | copy-start | bytes 4612
  1508.0 289.5 %copy-start.66 = (f32[384]{0:T(512)S(1)}, f32[384]{0:T(512)}, u32[]{:S(2)}) copy-start(f32[384]{0:T(512)} %copy-done.65) | copy-start | bytes 4612
  1508.0 289.5 %copy-start.57 = (f32[384]{0:T(512)S(1)}, f32[384]{0:T(512)}, u32[]{:S(2)}) copy-start(f32[384]{0:T(512)} %copy-done.56) | copy-start | bytes 4612
  1532.8 267.6 %copy-start.19 = (bf16[384,2048]{1,0:T(8,128)(2,1)S(1)}, bf16[384,2048]{1,0:T(8,128)(2,1)}, u32[]{:S(2)}) copy-start(bf16[384,2048]{1,0:T(8,128)(2,1)} %param.32) | copy-start | bytes 4718596
  1532.8 267.6 %copy-start.64 = (f32[384]{0:T(512)S(1)}, f32[384]{0:T(512)}, u32[]{:S(2)}) copy-start(f32[384]{0:T(512)} %copy-done.63) | copy-start | bytes 4612
  (54 other events, 218.6 us)
Sparse Core Ops, SparseCore 0:
  9.9 30.5 all-gather.12
  42.4 27.7 all-gather.14
  72.1 27.7 all-gather.16
  101.9 115.3 all-gather.10
  219.0 26.2 all-gather.18
  280.7 210.2 reduce-scatter.10
  492.8 55.2 all-gather.22
  550.3 115.3 all-gather.20
  667.3 113.4 all-gather.26
  782.5 54.0 all-gather.24
  906.2 211.8 reduce-scatter.14
  1120.3 111.7 reduce-scatter.12
  1241.0 115.8 all-gather.28
  1360.2 69.4 reduce-scatter.28
  1433.0 71.5 reduce-scatter.26
  1507.7 41.1 reduce-scatter.24
  1552.0 41.1 reduce-scatter.20
  1596.3 41.1 reduce-scatter.22
  1640.8 41.1 reduce-scatter.18
  1684.1 110.7 reduce-scatter.16
where the time goes:
time: 1860 us; the launch traced here: 1850 us
  waiting for transfers between devices  1350 us (73%)
  matrix products  296 us (16%)
  other arithmetic  97.5 us (5%)
  blocking collectives  66.5 us (4%)
  local copies, waits for them, and re-layouts  22.7 us (1%)
    reduce_scatter x1, waiting for transfers between devices, on_device(): lax.psum_scatter(row_dot(attended, full_out), 'tensor', scatter_dimension...  210 us
    reduce_scatter x1, waiting for transfers between devices, on_device(): lax.psum_scatter(back_dot(grad_pre, full_up), 'tensor', scatter_dimension...  180 us
    all_gather x1, waiting for transfers between devices, on_device(): h_two_full = lax.all_gather(h_two, 'tensor', axis=0, tiled=True)  118 us
    all_gather x1, waiting for transfers between devices, on_device(): h_one_full = lax.all_gather(h_one, 'tensor', axis=0, tiled=True)  117 us
    reduce_scatter x1, waiting for transfers between devices, on_device(): lax.psum_scatter((back_dot(grad_qkv[:, :head_cols], full_query) * score_s...  111 us
    reduce_scatter x1, waiting for transfers between devices, on_device(): lax.psum_scatter(row_dot(act_low, full_down).astype(jnp.bfloat16), 'tenso...  110 us
    all_gather x1, waiting for transfers between devices, on_device(): grad_y_full = lax.all_gather(cotangent, 'tensor', axis=0, tiled=True)  96 us
    dot_general x5, matrix products, back_dot(): lax.dot_general(left_side, right_side, (((1,), (1,)), ((), ())), preferre...  94.2 us
  transfers between devices with their start and end apart: 20, of which 17 were waited for; matrix products, arithmetic and copies ran while one was open for 17% of the time, Pallas kernels for 0%

commit v1 on v0

--- a/solution.py
+++ b/solution.py
@@ -8,6 +8,19 @@
 QBLK = 768
 EPS = 1e-05
 NEG = -1e30
+
+
+def collect(shard, axis, dim):
+    peers, mine, extent = (lax.axis_size(axis), lax.axis_index(axis), shard.shape[dim])
+    right = [(i, (i + 1) % peers) for i in range(peers)]
+    whole = jnp.zeros((*shard.shape[:dim], peers * extent, *shard.shape[dim + 1 :]), shard.dtype)
+    held = shard
+    for lap in range(peers):
+        owner = (mine - lap) % peers
+        whole = lax.dynamic_update_slice_in_dim(whole, held, owner * extent, axis=dim)
+        if lap < peers - 1:
+            held = lax.ppermute(held, axis, right)
+    return whole
 
 
 def layer_norm(values, norm_gain, norm_shift):
@@ -164,7 +177,7 @@
         + b_down.astype(jnp.float32)
     ).astype(jnp.bfloat16)
     grad_y = cotangent.astype(jnp.float32)
-    grad_y_full = lax.all_gather(cotangent, "tensor", axis=0, tiled=True)
+    grad_y_full = collect(cotangent, "tensor", 0)
     grad_down = left_dot(act_low, grad_y_full)
     grad_act = back_dot(grad_y_full, full_down)
     grad_pre = gelu_back(grad_act)[0].astype(jnp.bfloat16)

time: 1860 us -> 1780 us (0.957)
  waiting for transfers between devices: 1350 us -> 1260 us
    ppermute x0 -> x3, waiting for transfers between devices: none -> 141 us  [collect(): held = lax.ppermute(held, axis, right)]
    all_gather x1 -> x0, waiting for transfers between devices: 96 us -> none  [on_device(): grad_y_full = lax.all_gather(cotangent, 'tensor', axis=0, tiled=True)]
    all_gather x1, waiting for transfers between devices: 118 us -> 44.8 us  [on_device(): h_two_full = lax.all_gather(h_two, 'tensor', axis=0, tiled=True)]
    all_gather x1, waiting for transfers between devices: 49.4 us -> 0.01 us  [on_device(): lax.all_gather(w_up, 'dp', axis=0, tiled=True)]
    all_gather x1, waiting for transfers between devices: 55.8 us -> 36.8 us  [on_device(): lax.all_gather(w_down, 'dp', axis=1, tiled=True)]
  transfers between devices with their start and end apart: 20 -> 22, of which waited for: 17 -> 19; matrix products, arithmetic and copies ran while one was open for 17% -> 18% of each run, Pallas kernels for 0% -> 0%
where the time goes in v1:
time: 1780 us; the launch traced here: 1770 us
  waiting for transfers between devices  1260 us (71%)
  matrix products  292 us (16%)
  other arithmetic  100 us (6%)
  blocking collectives  65.2 us (4%)
  local copies, waits for them, and re-layouts  30.5 us (2%)
    reduce_scatter x1, waiting for transfers between devices, on_device(): lax.psum_scatter(row_dot(attended, full_out), 'tensor', scatter_dimension...  210 us
    reduce_scatter x1, waiting for transfers between devices, on_device(): lax.psum_scatter(back_dot(grad_pre, full_up), 'tensor', scatter_dimension...  180 us
    ppermute x3, waiting for transfers between devices, collect(): held = lax.ppermute(held, axis, right)  141 us
    all_gather x1, waiting for transfers between devices, on_device(): h_one_full = lax.all_gather(h_one, 'tensor', axis=0, tiled=True)  117 us
    reduce_scatter x1, waiting for transfers between devices, on_device(): lax.psum_scatter((back_dot(grad_qkv[:, :head_cols], full_query) * score_s...  111 us
    reduce_scatter x1, waiting for transfers between devices, on_device(): lax.psum_scatter(row_dot(act_low, full_down).astype(jnp.bfloat16), 'tenso...  111 us
    dot_general x5, matrix products, back_dot(): lax.dot_general(left_side, right_side, (((1,), (1,)), ((), ())), preferre...  92.1 us
    all_gather x1, waiting for transfers between devices, on_device(): grad_mix_full = lax.all_gather(grad_mix, 'tensor', axis=0, tiled=True)  76.2 us
  transfers between devices with their start and end apart: 22, of which 19 were waited for; matrix products, arithmetic and copies ran while one was open for 18% of the time, Pallas kernels for 0%

profile of v1, /device:TPU:0, one launch (start us, length us, event | category | flops | bytes accessed | tf_op | source)
XLA Modules:
  0.0 1773.2 jit_solution(13464957446907993665)
XLA Ops:
  22.3 18.1 %all-gather.12.cloned.1.call-done = bf16[2048,512]{1,0:T(8,128)(2,1)} async-done(((bf16[256,512]{1,0:T(8,128)(2,1)}), bf16[2048,512]{1,0:T(8,128)(2,1)}) %all-gather.12.cloned.1.call-update) | async-done | bytes 2097168 | tf_op jit(solution)/shard_map/all_gather | solution.py:116
  40.5 29.7 %all-gather.14.cloned.1.call-done = bf16[2048,512]{1,0:T(8,128)(2,1)} async-done(((bf16[256,512]{1,0:T(8,128)(2,1)}), bf16[2048,512]{1,0:T(8,128)(2,1)}) %all-gather.14.cloned.1.call-update) | async-done | bytes 2097168 | tf_op jit(solution)/shard_map/all_gather | solution.py:117
  70.1 29.7 %all-gather.16.cloned.1.call-done = bf16[2048,512]{1,0:T(8,128)(2,1)} async-done(((bf16[256,512]{1,0:T(8,128)(2,1)}), bf16[2048,512]{1,0:T(8,128)(2,1)}) %all-gather.16.cloned.1.call-update) | async-done | bytes 2097168 | tf_op jit(solution)/shard_map/all_gather | solution.py:118
  99.8 117.4 %all-gather.10.cloned.1.call-done = bf16[1536,2048]{1,0:T(8,128)(2,1)} async-done(((bf16[384,2048]{1,0:T(8,128)(2,1)}), bf16[1536,2048]{1,0:T(8,128)(2,1)}) %all-gather.10.cloned.1.call-update) | async-done | bytes 6291472 | tf_op jit(solution)/shard_map/all_gather | solution.py:132
  217.2 17.0 fusion.99
  237.2 3.9 fusion.60
  251.1 5.1 fusion
  257.9 9.1 fusion.79
  267.2 8.5 fusion.101
  276.6 209.5 %reduce-scatter.11.cloned.1.call-done = f32[384,2048]{1,0:T(8,128)} async-done(((f32[1536,2048]{1,0:T(8,128)}), f32[384,2048]{1,0:T(8,128)}) %reduce-scatter.11.cloned.1.call-update) | async-done | bytes 3145744 | tf_op jit(solution)/shard_map/reduce_scatter | solution.py:158
  494.9 36.4 %collective-permute-done = bf16[384,2048]{1,0:T(8,128)(2,1)S(1)} collective-permute-done((bf16[384,2048]{1,0:T(8,128)(2,1)S(1)}, bf16[384,2048]{1,0:T(8,128)(2,1)S(1)}, u32[]{:S(2)}, u32[]{:S(2)}) %collective-permute-start) | collective-permute-done | bytes 1572896 | tf_op jit(solution)/shard_map/ppermute | solution.py:22
  531.3 48.6 %collective-permute-done.1 = bf16[384,2048]{1,0:T(8,128)(2,1)} collective-permute-done((bf16[384,2048]{1,0:T(8,128)(2,1)S(1)}, bf16[384,2048]{1,0:T(8,128)(2,1)}, u32[]{:S(2)}, u32[]{:S(2)}) %collective-permute-start.1) | collective-permute-done | bytes 1572896 | tf_op jit(solution)/shard_map/ppermute | solution.py:22
  579.8 11.5 collective-permute-start.2
  600.1 56.1 %collective-permute-done.2 = bf16[384,2048]{1,0:T(8,128)(2,1)} collective-permute-done((bf16[384,2048]{1,0:T(8,128)(2,1)}, bf16[384,2048]{1,0:T(8,128)(2,1)}, u32[]{:S(2)}, u32[]{:S(2)}) %collective-permute-start.2) | collective-permute-done | bytes 1572896 | tf_op jit(solution)/shard_map/ppermute | solution.py:22
  658.9 44.8 %all-gather.20.cloned.1.call-done = bf16[1536,2048]{1,0:T(8,128)(2,1)} async-done(((bf16[384,2048]{1,0:T(8,128)(2,1)}), bf16[1536,2048]{1,0:T(8,128)(2,1)}) %all-gather.20.cloned.1.call-update) | async-done | bytes 6291472 | tf_op jit(solution)/shard_map/all_gather | solution.py:165
  703.8 19.1 %fusion.102 = f32[1536,2048]{1,0:T(8,128)} fusion(bf16[1536,2048]{1,0:T(8,128)(2,1)} %all-gather.20.cloned.1.call-done, bf16[2048,2048]{1,0:T(8,128)(2,1)} %all-gather.22.cloned.1.call-done), kind=kOutput, calls=%fused_computation.167 | convolution fusion | flops 12884901888 | bytes 27262976 | tf_op jit(solution)/shard_map/dot_general | solution.py:38
  722.9 36.8 %all-gather.24.cloned.1.call-done = bf16[2048,2048]{1,0:T(8,128)(2,1)} async-done(((bf16[2048,256]{1,0:T(8,128)(2,1)}), bf16[2048,2048]{1,0:T(8,128)(2,1)}) %all-gather.24.cloned.1.call-update) | async-done | bytes 8388624 | tf_op jit(solution)/shard_map/all_gather | solution.py:121
  759.7 48.6 %convert_reduce_fusion = (f32[2048]{0:T(1024)}, bf16[1536,2048]{1,0:T(8,128)(2,1)S(1)}, f32[1536,2048]{1,0:T(8,128)}) fusion(f32[1536,2048]{1,0:T(8,128)} %fusion.102, f32[2048]{0:T(1024)S(1)} %convert_element_type.195, bf16[1536,2048]{1,0:T(8,128)(2,1)} %constant_dynamic-update-slice_fusion, bf16[2048,2048]{1,0:T(8,128)(2,1)} %all-gather.24.cloned.1.call-done), kind=kOutput, calls=%fused_computation.9 | convolution fusion | flops 13120829440 | bytes 46153728 | tf_op jit(solution)/shard_map/dot_general | solution.py:48
  810.9 16.1 fusion.103
  827.1 10.7 multiply_convert_fusion.1
  840.6 17.5 convolution_convert_fusion.2
  858.8 180.4 %reduce-scatter.15.cloned.1.call-done = f32[384,2048]{1,0:T(8,128)} async-done(((f32[1536,2048]{1,0:T(8,128)}), f32[384,2048]{1,0:T(8,128)}) %reduce-scatter.15.cloned.1.call-update) | async-done | bytes 3145744 | tf_op jit(solution)/shard_map/reduce_scatter | solution.py:186
  1042.7 110.6 %reduce-scatter.13.cloned.1.call-done = bf16[384,2048]{1,0:T(8,128)(2,1)} async-done(((bf16[1536,2048]{1,0:T(8,128)(2,1)}), bf16[384,2048]{1,0:T(8,128)(2,1)}) %reduce-scatter.13.cloned.1.call-update) | async-done | bytes 1572880 | tf_op jit(solution)/shard_map/reduce_scatter | solution.py:171
  1153.3 4.8 fusion.92
  1162.1 19.4 %convolution_convert_fusion = bf16[2048,2048]{1,0:T(8,128)(2,1)} fusion(bf16[1536,2048]{1,0:T(8,128)(2,1)} %copy-done.29, bf16[1536,2048]{1,0:T(8,128)(2,1)} %constant_dynamic-update-slice_fusion), kind=kOutput, calls=%fused_computation.39 | convolution fusion | flops 12889096192 | bytes 20971520 | tf_op jit(solution)/shard_map/dot_general | solution.py:42
  1181.7 19.3 %convolution_convert_fusion.1 = bf16[2048,2048]{1,0:T(8,128)(2,1)} fusion(bf16[1536,2048]{1,0:T(8,128)(2,1)} %all-gather.20.cloned.1.call-done, bf16[1536,2048]{1,0:T(8,128)(2,1)} %copy-done.80), kind=kOutput, calls=%fused_computation.40 | convolution fusion | flops 12889096192 | bytes 20971520 | tf_op jit(solution)/shard_map/dot_general | solution.py:42
  1201.8 76.2 %all-gather.26.cloned.1.call-done = bf16[1536,2048]{1,0:T(8,128)(2,1)} async-done(((bf16[384,2048]{1,0:T(8,128)(2,1)}), bf16[1536,2048]{1,0:T(8,128)(2,1)}) %all-gather.26.cloned.1.call-update) | async-done | bytes 6291472 | tf_op jit(solution)/shard_map/all_gather | solution.py:194
  1278.0 6.9 convolution_convert_fusion.4
  1285.9 9.6 multiply_reduce_fusion.1
  1295.5 10.9 multiply_convert_fusion.2
  1306.4 4.4 fusion.77
  1313.6 17.0 multiply_reduce_fusion
  1330.6 14.8 multiply_convert_fusion
  1348.0 4.1 fusion.78
  1352.1 4.4 fusion.72
  1356.5 7.4 convolution_convert_fusion.3
  1364.0 12.9 convert_reduce_fusion.5
  1377.1 17.0 fusion.100
  1397.1 4.2 fusion.39
  1401.4 12.2 fusion.40
  1413.6 8.2 add_convert_fusion
  1430.4 23.2 %all-reduce.3 = (f32[512]{0:T(512)}, f32[512]{0:T(512)}, f32[2048]{0:T(1024)}) all-reduce(f32[512]{0:T(512)S(1)} %multiply_bitcast_fusion, f32[512]{0:T(512)S(1)} %bitcast.105, f32[2048]{0:T(1024)S(1)} %copy-done.70), channel_id=1, replica_groups=mesh['dp'=8,'tensor'=4] {'dp'}, use_global_device_ids=true, to_apply=%region_24.25 | all-reduce | flops 3072 | bytes 24576 | tf_op jit(solution)/shard_map/psum | solution.py:258
  1453.6 16.5 reduce-scatter.25.cloned.1.call-done
  1471.9 42.5 %reduce-scatter.21.cloned.1.call-done = bf16[256,512]{1,0:T(8,128)(2,1)} async-done(((bf16[2048,512]{1,0:T(8,128)(2,1)}), bf16[256,512]{1,0:T(8,128)(2,1)}) %reduce-scatter.21.cloned.1.call-update) | async-done | bytes 262160 | tf_op jit(solution)/shard_map/reduce_scatter | solution.py:242
  1516.2 42.5 %reduce-scatter.23.cloned.1.call-done = bf16[256,512]{1,0:T(8,128)(2,1)} async-done(((bf16[2048,512]{1,0:T(8,128)(2,1)}), bf16[256,512]{1,0:T(8,128)(2,1)}) %reduce-scatter.23.cloned.1.call-update) | async-done | bytes 262160 | tf_op jit(solution)/shard_map/reduce_scatter | solution.py:245
  1560.5 42.5 %reduce-scatter.19.cloned.1.call-done = bf16[256,512]{1,0:T(8,128)(2,1)} async-done(((bf16[2048,512]{1,0:T(8,128)(2,1)}), bf16[256,512]{1,0:T(8,128)(2,1)}) %reduce-scatter.19.cloned.1.call-update) | async-done | bytes 262160 | tf_op jit(solution)/shard_map/reduce_scatter | solution.py:239
  1604.8 111.3 %reduce-scatter.17.cloned.1.call-done = bf16[384,2048]{1,0:T(8,128)(2,1)} async-done(((bf16[1536,2048]{1,0:T(8,128)(2,1)}), bf16[384,2048]{1,0:T(8,128)(2,1)}) %reduce-scatter.17.cloned.1.call-update) | async-done | bytes 1572880 | tf_op jit(solution)/shard_map/reduce_scatter | solution.py:227
  1724.5 42.0 %all-reduce.2 = (f32[2048]{0:T(1024)}, f32[2048]{0:T(1024)}, f32[2048]{0:T(1024)}, f32[2048]{0:T(1024)}, f32[2048]{0:T(1024)}, /*index=5*/f32[2048]{0:T(1024)}) all-reduce(f32[2048]{0:T(1024)S(1)} %get-tuple-element.83, f32[2048]{0:T(1024)S(1)} %get-tuple-element.86, ...), channel_id=1, replica_groups=mesh['dp'=8,'tensor'=4] {'dp','tensor'}, use_global_device_ids=true, to_apply=%region_19.20 | all-reduce | flops 12288 | bytes 98304 | tf_op jit(solution)/shard_map/psum | solution.py:262
  (275 shorter events, 98.6 us)
Async XLA Ops:
  7.2 33.2 %all-gather.12.cloned.1.call-start = ((), (), s32[]{:S(2)}) async-start(), calls=%async_computation.11 | async-start | bytes 2359296 | tf_op jit(solution)/shard_map/all_gather | solution.py:116
  8.0 62.2 %all-gather.14.cloned.1.call-start = ((), (), s32[]{:S(2)}) async-start(), calls=%async_computation.12 | async-start | bytes 2359296 | tf_op jit(solution)/shard_map/all_gather | solution.py:117
  8.7 91.1 %all-gather.16.cloned.1.call-start = ((), (), s32[]{:S(2)}) async-start(), calls=%async_computation.13 | async-start | bytes 2359296 | tf_op jit(solution)/shard_map/all_gather | solution.py:118
  9.4 207.8 %all-gather.10.cloned.1.call-start = ((), (), s32[]{:S(2)}) async-start(), calls=%async_computation.10 | async-start | bytes 7864320 | tf_op jit(solution)/shard_map/all_gather | solution.py:132
  19.0 248.2 %all-gather.18.cloned.1.call-start = ((), (), s32[]{:S(2)}) async-start(), calls=%async_computation.14 | async-start | bytes 2359296 | tf_op jit(solution)/shard_map/all_gather | solution.py:119
  19.5 466.6 %reduce-scatter.11.cloned.1.call-start = ((), (), s32[]{:S(2)}) async-start(), calls=%async_computation.15 | async-start | bytes 15728640 | tf_op jit(solution)/shard_map/reduce_scatter | solution.py:158
  20.1 224.7 %copy-start.13 = (pred[768,768]{0,1:T(8,128)(4,1)}, pred[768,768]{0,1:T(8,128)(4,1)S(1)}, u32[]{:S(2)}) copy-start(pred[768,768]{0,1:T(8,128)(4,1)S(1)} %fusion.69) | copy-start | bytes 1769476
  22.3 235.2 %copy-start.6 = (pred[768,1536]{1,0:T(8,128)(4,1)}, pred[768,1536]{1,0:T(8,128)(4,1)S(1)}, u32[]{:S(2)}) copy-start(pred[768,1536]{1,0:T(8,128)(4,1)S(1)} %fusion.36) | copy-start | bytes 3538948
  241.1 16.4 copy-start.15
  275.7 210.4 %copy-start.4 = (bf16[384,2048]{1,0:T(8,128)(2,1)S(1)}, bf16[384,2048]{1,0:T(8,128)(2,1)}, u32[]{:S(2)}) copy-start(bf16[384,2048]{1,0:T(8,128)(2,1)} %param.30) | copy-start | bytes 4718596
  275.8 383.2 %all-gather.22.cloned.1.call-start = ((), (), s32[]{:S(2)}) async-start(), calls=%async_computation.17 | async-start | bytes 9437184 | tf_op jit(solution)/shard_map/all_gather | solution.py:120
  276.5 427.3 %all-gather.20.cloned.1.call-start = ((), (), s32[]{:S(2)}) async-start(), calls=%async_computation.16 | async-start | bytes 7864320 | tf_op jit(solution)/shard_map/all_gather | solution.py:165
  276.6 215.9 %copy-start.42 = (f32[2048]{0:T(1024)}, f32[2048]{0:T(1024)S(1)}, u32[]{:S(2)}) copy-start(f32[2048]{0:T(1024)S(1)} %convert_element_type.192) | copy-start | bytes 24580
  488.5 102.8 %copy-start.74 = (bf16[2048]{0:T(1024)(128)(2,1)S(1)}, bf16[2048]{0:T(1024)(128)(2,1)}, u32[]{:S(2)}) copy-start(bf16[2048]{0:T(1024)(128)(2,1)} %param.45) | copy-start | bytes 12292
  492.5 267.1 %all-gather.24.cloned.1.call-start = ((), (), s32[]{:S(2)}) async-start(), calls=%async_computation.18 | async-start | bytes 9437184 | tf_op jit(solution)/shard_map/all_gather | solution.py:121
  493.3 545.9 %reduce-scatter.15.cloned.1.call-start = ((), (), s32[]{:S(2)}) async-start(), calls=%async_computation.20 | async-start | bytes 15728640 | tf_op jit(solution)/shard_map/reduce_scatter | solution.py:186
  493.3 37.9 %collective-permute-start = (bf16[384,2048]{1,0:T(8,128)(2,1)S(1)}, bf16[384,2048]{1,0:T(8,128)(2,1)S(1)}, u32[]{:S(2)}, u32[]{:S(2)}) collective-permute-start(bf16[384,2048]{1,0:T(8,128)(2,1)S(1)} %copy-done.18), channel_id=1, source_target_pairs={{0,1},{1,2},{2,3},{3,0},{4,5},{5,6},{6,7},{7,4},{8,9},{9,10},{10,1... | collective-permute-start | bytes 4718600 | tf_op jit(solution)/shard_map/ppermute | solution.py:22
  531.3 48.6 %collective-permute-start.1 = (bf16[384,2048]{1,0:T(8,128)(2,1)S(1)}, bf16[384,2048]{1,0:T(8,128)(2,1)}, u32[]{:S(2)}, u32[]{:S(2)}) collective-permute-start(bf16[384,2048]{1,0:T(8,128)(2,1)S(1)} %collective-permute-done), channel_id=1, source_target_pairs={{0,1},{1,2},{2,3},{3,0},{4,5},{5,6},{6,7},{7,4},{8,9},{9,10},{10,1... | collective-permute-start | bytes 4718600 | tf_op jit(solution)/shard_map/ppermute | solution.py:22
  579.8 76.4 %collective-permute-start.2 = (bf16[384,2048]{1,0:T(8,128)(2,1)}, bf16[384,2048]{1,0:T(8,128)(2,1)}, u32[]{:S(2)}, u32[]{:S(2)}) collective-permute-start(bf16[384,2048]{1,0:T(8,128)(2,1)} %collective-permute-done.1), channel_id=1, source_target_pairs={{0,1},{1,2},{2,3},{3,0},{4,5},{5,6},{6,7},{7,4},{8,9},{9,10},{10,1... | collective-permute-start | bytes 4718600 | tf_op jit(solution)/shard_map/ppermute | solution.py:22
  759.7 51.3 %copy-start.78 = (bf16[2048,2048]{1,0:T(8,128)(2,1)S(1)}, bf16[2048,2048]{1,0:T(8,128)(2,1)}, u32[]{:S(2)}) copy-start(bf16[2048,2048]{1,0:T(8,128)(2,1)} %all-gather.22.cloned.1.call-done) | copy-start | bytes 25165828
  827.1 326.2 %reduce-scatter.13.cloned.1.call-start = ((), (), s32[]{:S(2)}) async-start(), calls=%async_computation.19 | async-start | bytes 7864320 | tf_op jit(solution)/shard_map/reduce_scatter | solution.py:171
  858.1 181.1 %copy-start.3 = (f32[384,2048]{1,0:T(8,128)S(1)}, f32[384,2048]{1,0:T(8,128)}, u32[]{:S(2)}) copy-start(f32[384,2048]{1,0:T(8,128)} %copy-done.2) | copy-start | bytes 9437188
  858.1 181.1 %copy-start.43 = (f32[2048]{0:T(1024)S(1)}, f32[2048]{0:T(1024)}, u32[]{:S(2)}) copy-start(f32[2048]{0:T(1024)} %copy-done.42) | copy-start | bytes 24580
  858.1 181.1 %copy-start.52 = (f32[384]{0:T(512)S(1)}, f32[384]{0:T(512)}, u32[]{:S(2)}) copy-start(f32[384]{0:T(512)} %copy-done.51) | copy-start | bytes 4612
  858.1 181.1 %copy-start.63 = (f32[384]{0:T(512)S(1)}, f32[384]{0:T(512)}, u32[]{:S(2)}) copy-start(f32[384]{0:T(512)} %copy-done.62) | copy-start | bytes 4612
  858.1 184.6 %copy-start.69 = (f32[384]{0:T(512)S(1)}, f32[384]{0:T(512)}, u32[]{:S(2)}) copy-start(f32[384]{0:T(512)} %copy-done.68) | copy-start | bytes 4612
  858.1 419.9 %all-gather.26.cloned.1.call-start = ((), (), s32[]{:S(2)}) async-start(), calls=%async_computation.21 | async-start | bytes 7864320 | tf_op jit(solution)/shard_map/all_gather | solution.py:194
  1162.0 259.9 %reduce-scatter.29.cloned.1.call-start = ((), (), s32[]{:S(2)}) async-start(), calls=%async_computation.28 | async-start | bytes 9437184 | tf_op jit(solution)/shard_map/reduce_scatter | solution.py:254
  1181.5 244.3 %reduce-scatter.27.cloned.1.call-start = ((), (), s32[]{:S(2)}) async-start(), calls=%async_computation.27 | async-start | bytes 9437184 | tf_op jit(solution)/shard_map/reduce_scatter | solution.py:251
  1201.1 269.0 %reduce-scatter.25.cloned.1.call-start = ((), (), s32[]{:S(2)}) async-start(), calls=%async_computation.26 | async-start | bytes 2359296 | tf_op jit(solution)/shard_map/reduce_scatter | solution.py:248
  1201.8 84.1 %copy-start.14 = (pred[768,768]{0,1:T(8,128)(4,1)S(1)}, pred[768,768]{0,1:T(8,128)(4,1)}, u32[]{:S(2)}) copy-start(pred[768,768]{0,1:T(8,128)(4,1)} %copy-done.13) | copy-start | bytes 1769476
  1201.8 84.0 %copy-start.33 = (bf16[768,512]{0,1:T(8,128)(2,1)S(1)}, bf16[768,512]{0,1:T(8,128)(2,1)}, u32[]{:S(2)}) copy-start(bf16[768,512]{0,1:T(8,128)(2,1)} %copy-done.32) | copy-start | bytes 2359300
  1330.6 14.8 copy-start.23
  1330.6 14.8 copy-start.28
  1364.0 13.0 copy-start.24
  1364.0 13.0 copy-start.27
  1376.9 137.5 %reduce-scatter.21.cloned.1.call-start = ((), (), s32[]{:S(2)}) async-start(), calls=%async_computation.24 | async-start | bytes 2359296 | tf_op jit(solution)/shard_map/reduce_scatter | solution.py:242
  1377.1 17.0 copy-start.38
  1396.5 162.2 %reduce-scatter.23.cloned.1.call-start = ((), (), s32[]{:S(2)}) async-start(), calls=%async_computation.25 | async-start | bytes 2359296 | tf_op jit(solution)/shard_map/reduce_scatter | solution.py:245
  1397.0 205.9 %reduce-scatter.19.cloned.1.call-start = ((), (), s32[]{:S(2)}) async-start(), calls=%async_computation.23 | async-start | bytes 2359296 | tf_op jit(solution)/shard_map/reduce_scatter | solution.py:239
  1401.3 314.8 %reduce-scatter.17.cloned.1.call-start = ((), (), s32[]{:S(2)}) async-start(), calls=%async_computation.22 | async-start | bytes 7864320 | tf_op jit(solution)/shard_map/reduce_scatter | solution.py:227
  1421.8 294.3 %copy-start.5 = (bf16[384,2048]{1,0:T(8,128)(2,1)S(1)}, bf16[384,2048]{1,0:T(8,128)(2,1)}, u32[]{:S(2)}) copy-start(bf16[384,2048]{1,0:T(8,128)(2,1)} %param.30) | copy-start | bytes 4718596
  1421.9 294.3 %copy-start.41 = (f32[2048]{0:T(1024)S(1)}, f32[2048]{0:T(1024)}, u32[]{:S(2)}) copy-start(f32[2048]{0:T(1024)} %copy-done.40) | copy-start | bytes 24580
  1421.9 294.2 %copy-start.50 = (f32[384]{0:T(512)S(1)}, f32[384]{0:T(512)}, u32[]{:S(2)}) copy-start(f32[384]{0:T(512)} %copy-done.49) | copy-start | bytes 4612
  1424.7 293.9 %copy-start.67 = (f32[384]{0:T(512)S(1)}, f32[384]{0:T(512)}, u32[]{:S(2)}) copy-start(f32[384]{0:T(512)} %copy-done.66) | copy-start | bytes 4612
  1424.7 293.9 %copy-start.58 = (f32[384]{0:T(512)S(1)}, f32[384]{0:T(512)}, u32[]{:S(2)}) copy-start(f32[384]{0:T(512)} %copy-done.57) | copy-start | bytes 4612
  1428.6 293.0 %copy-start.20 = (bf16[384,2048]{1,0:T(8,128)(2,1)S(1)}, bf16[384,2048]{1,0:T(8,128)(2,1)}, u32[]{:S(2)}) copy-start(bf16[384,2048]{1,0:T(8,128)(2,1)} %param.32) | copy-start | bytes 4718596
  1428.6 293.0 %copy-start.65 = (f32[384]{0:T(512)S(1)}, f32[384]{0:T(512)}, u32[]{:S(2)}) copy-start(f32[384]{0:T(512)} %copy-done.64) | copy-start | bytes 4612
  (58 other events, 290.0 us)
Sparse Core Ops, SparseCore 0:
  9.9 30.4 all-gather.11
  42.3 27.7 all-gather.13
  72.0 27.7 all-gather.15
  101.8 115.3 all-gather.9
  218.9 26.2 all-gather.17
  275.9 210.2 reduce-scatter.10
  488.0 55.2 all-gather.21
  545.5 158.1 all-gather.19
  705.6 53.9 all-gather.23
  827.2 211.8 reduce-scatter.14
  1041.4 111.7 reduce-scatter.12
  1162.2 115.8 all-gather.25
  1281.5 69.4 reduce-scatter.28
  1354.3 71.4 reduce-scatter.26
  1428.9 41.1 reduce-scatter.24
  1473.3 41.0 reduce-scatter.20
  1517.5 41.1 reduce-scatter.22
  1561.8 41.1 reduce-scatter.18
  1605.3 110.7 reduce-scatter.16
